TPU v7x, 32 devices: a whole 2x2x4 slice. The times are simulated.
32 devices in a mesh: groups: 2 (over y), pool: 8 (over z, x), heads: 2 (over core).
Axes of the slice: x: 2, y: 2, z: 4, core: 2. Of those that a mesh axis runs over, the one named last changes fastest.
Arguments:
- hidden_in: bfloat16 [32, 8192], P('groups'), parts along dimension 0, may hold values from -50 to 50
- key_cache: bfloat16 [32, 8, 4096, 128], P('groups', 'heads', 'pool'), parts along dimension 0, may hold values from -200 to 200
- value_cache: bfloat16 [32, 8, 4096, 128], P('groups', 'heads', 'pool'), parts along dimension 0, may hold values from -6 to 6
- positions: int32 [3, 32, 4096], P(None, 'groups', 'pool'), parts along dimension 1, may hold values from 0 to 4095, as said below
- query_pos: int32 [3, 32], P(None, 'groups'), parts along dimension 1, may hold values from 4096 to 8207
- lengths: int32 [32], P('groups'), parts along dimension 0, may hold values from 1024 to 4096, as said below
- query_weight: bfloat16 [8192, 8192], P('pool', 'heads'), may hold values from -0.0625 to 0.0625
- key_weight: bfloat16 [8192, 1024], P('pool', 'heads'), may hold values from -0.16503906 to 0.16503906
- value_weight: bfloat16 [8192, 1024], P('pool', 'heads'), may hold values from -0.16503906 to 0.16503906
- out_weight: bfloat16 [8192, 8192], P('heads', 'pool'), may hold values from -0.5 to 0.5
- gate_weight: bfloat16 [8192, 14848], P(None, ('pool', 'heads')), may hold values from -0.0625 to 0.0625
- up_weight: bfloat16 [8192, 14848], P(None, ('pool', 'heads')), may hold values from -0.0625 to 0.0625
- down_weight: bfloat16 [14848, 8192], P(('pool', 'heads')), may hold values from -0.0625 to 0.0625
Outputs:
- output: bfloat16 [32, 8192], P('groups', 'pool'), parts along dimension 0
There are 2 independent parts, one for each index of `groups`. A program takes and returns all parts, laid end to end along the dimension named above; an argument that names none is the same for every part. Nothing has to cross between parts.
Inputs may be any that keep to these rules, and one draw needn't show every extreme that they name: `positions`: text tokens carry three equal ids; one prompt is text only. `lengths`: some prompt fills all 4096 slots.
All inputs are finite; a program needn't handle non-finite values.
Results may differ from a plain program's by a relative error of at most 0.007.
The roundings to bfloat16 on the way count: a program that leaves them out, or rounds other values in their place, can miss the bound.
Values may be sent and summed in bfloat16 or wider, within the bound.
A program may use at most 192 MiB of HBM per device.

v0:
```python
import math

import jax
import jax.numpy as jnp
from jax import lax
from jax.sharding import PartitionSpec as P

D = 8192
HEADS = 64
KV_HEADS = 8
HD = 128
PROMPTS = 16


EPS = 1e-06
THETA = 1000000.0


def angle_tables(triple):
    half_dim = HD // 2
    column = jnp.arange(half_dim)
    first_end = HD // 8
    second_end = first_end + 3 * HD // 16
    chosen = jnp.where(
        column < first_end,
        triple[0][..., None],
        jnp.where(column < second_end, triple[1][..., None], triple[2][..., None]),
    )
    inverse = jnp.exp(column.astype(jnp.float32) * (-2.0 * math.log(THETA) / HD))
    angles = chosen.astype(jnp.float32) * inverse
    return (jnp.cos(angles), jnp.sin(angles))


def rotate(values, cos_table, sin_table):
    half_dim = values.shape[-1] // 2
    lower_half = values[..., :half_dim]
    upper_half = values[..., half_dim:]
    return jnp.concatenate(
        [
            lower_half * cos_table - upper_half * sin_table,
            upper_half * cos_table + lower_half * sin_table,
        ],
        -1,
    )


def normalize(values):
    return values * lax.rsqrt(jnp.mean(values * values, -1, keepdims=True) + EPS)


def prepare(projected_rows, item_ids, local_heads, query_pos):
    query_width = projected_rows.shape[1] - 2 * HD
    prompt_ids = item_ids // local_heads
    triple = query_pos[:, prompt_ids]
    cos_table, sin_table = angle_tables(triple)
    item_count = projected_rows.shape[0]
    raw_queries = projected_rows[:, :query_width].reshape(item_count, query_width // HD, HD)
    queries = rotate(raw_queries, cos_table[:, None], sin_table[:, None]).astype(jnp.bfloat16)
    own_keys = rotate(
        projected_rows[:, query_width : query_width + HD], cos_table, sin_table
    ).astype(jnp.bfloat16)
    own_values = projected_rows[:, query_width + HD :].astype(jnp.bfloat16)
    return (queries, own_keys, own_values)


def partial_softmax(queries, key_rows, value_rows, item_lengths, offset):
    scores = jnp.einsum(
        "igd,isd->igs", queries, key_rows, preferred_element_type=jnp.float32
    ) * HD ** (-0.5)
    slot_index = offset + jnp.arange(key_rows.shape[1])
    valid_mask = slot_index[None, None, :] < item_lengths[:, None, None]
    scores = jnp.where(valid_mask, scores, -1e30)
    peak_score = jnp.max(scores, -1)
    weights = jnp.where(valid_mask, jnp.exp(scores - peak_score[..., None]), 0.0)
    weighted = jnp.einsum("igs,isd->igd", weights, value_rows.astype(jnp.float32))
    return (peak_score, jnp.sum(weights, -1), weighted.reshape(queries.shape[0], -1))


def combine(peaks, totals, weighted, own_score, own_values):
    item_count, source_count, group_size = peaks.shape
    top_score = jnp.maximum(jnp.max(peaks, 1), own_score)
    factor = jnp.exp(peaks - top_score[:, None])
    own_weight = jnp.exp(own_score - top_score)
    denominator = jnp.sum(totals * factor, 1) + own_weight
    numerator = jnp.sum(
        weighted.reshape(item_count, source_count, group_size, HD) * factor[..., None], 1
    )
    numerator = numerator + own_weight[..., None] * own_values.astype(jnp.float32)[:, None, :]
    return (
        (numerator / denominator[..., None])
        .reshape(item_count, group_size * HD)
        .astype(jnp.bfloat16)
    )


def per_device(
    hidden_in,
    key_cache,
    value_cache,
    positions,
    query_pos,
    lengths,
    query_weight,
    key_weight,
    value_weight,
    out_weight,
    gate_weight,
    up_weight,
    down_weight,
):
    pool_index = lax.axis_index("pool")
    pool_size = lax.axis_size("pool")
    local_heads = key_cache.shape[1]
    group_size = HEADS // KV_HEADS
    query_width = group_size * HD
    all_items = PROMPTS * local_heads
    my_count = all_items // pool_size
    my_start = pool_index * my_count
    seq_local = key_cache.shape[2]
    block_cols = D // pool_size
    normed = normalize(hidden_in.astype(jnp.float32)).astype(jnp.bfloat16)
    normed_cols = lax.dynamic_slice_in_dim(normed, pool_index * block_cols, block_cols, 1)
    term = jnp.concatenate(
        [
            jnp.dot(normed_cols, query_weight, preferred_element_type=jnp.float32).reshape(
                PROMPTS, local_heads, query_width
            ),
            jnp.dot(normed_cols, key_weight, preferred_element_type=jnp.float32).reshape(
                PROMPTS, local_heads, HD
            ),
            jnp.dot(normed_cols, value_weight, preferred_element_type=jnp.float32).reshape(
                PROMPTS, local_heads, HD
            ),
        ],
        2,
    ).reshape(all_items, query_width + 2 * HD)
    cos_table, sin_table = angle_tables(positions)
    rotated = rotate(key_cache.astype(jnp.float32), cos_table[:, None], sin_table[:, None]).astype(
        jnp.bfloat16
    )
    rotated = rotated.reshape(all_items, seq_local, HD)
    value_rows = value_cache.reshape(all_items, seq_local, HD)
    item_lengths = jnp.repeat(lengths, local_heads)
    projected_all = lax.psum(term, "pool")
    all_queries, all_keys, all_values = prepare(
        projected_all, jnp.arange(all_items), local_heads, query_pos
    )
    local_peaks, local_totals, local_weighted = partial_softmax(
        all_queries, rotated, value_rows, item_lengths, pool_index * seq_local
    )
    peaks, totals, weighted = (
        lax.all_to_all(local_peaks[:, None], "pool", split_axis=0, concat_axis=1, tiled=True),
        lax.all_to_all(local_totals[:, None], "pool", split_axis=0, concat_axis=1, tiled=True),
        lax.all_to_all(local_weighted[:, None], "pool", split_axis=0, concat_axis=1, tiled=True),
    )
    queries = lax.dynamic_slice_in_dim(all_queries, my_start, my_count, 0)
    own_keys = lax.dynamic_slice_in_dim(all_keys, my_start, my_count, 0)
    own_values = lax.dynamic_slice_in_dim(all_values, my_start, my_count, 0)
    own_score = jnp.einsum(
        "igd,id->ig", queries, own_keys, preferred_element_type=jnp.float32
    ) * HD ** (-0.5)
    attended = combine(peaks, totals, weighted, own_score, own_values)
    gathered = lax.all_gather(attended, "pool", axis=0, tiled=True).reshape(
        PROMPTS, local_heads * query_width
    )
    attn_out = lax.psum(jnp.dot(gathered, out_weight, preferred_element_type=jnp.float32), "heads")
    hidden_cols = lax.dynamic_slice_in_dim(hidden_in, pool_index * block_cols, block_cols, 1)
    mid_state = (hidden_cols.astype(jnp.float32) + attn_out).astype(jnp.bfloat16)
    squares = lax.psum(jnp.sum(jnp.square(mid_state.astype(jnp.float32)), -1), "pool")
    whole_state = lax.all_gather(mid_state, "pool", axis=1, tiled=True)
    inverse = lax.rsqrt(squares / D + EPS)
    normed_state = (whole_state.astype(jnp.float32) * inverse[:, None]).astype(jnp.bfloat16)
    gate_values = jnp.dot(normed_state, gate_weight, preferred_element_type=jnp.float32)
    up_values = jnp.dot(normed_state, up_weight, preferred_element_type=jnp.float32)
    active = (jax.nn.silu(gate_values) * up_values).astype(jnp.bfloat16)
    partial_out = jnp.dot(active, down_weight, preferred_element_type=jnp.float32)
    mlp_cols = lax.psum_scatter(partial_out, "pool", scatter_dimension=1, tiled=True)
    mlp_cols = lax.psum(mlp_cols, "heads")
    return (mid_state.astype(jnp.float32) + mlp_cols).astype(jnp.bfloat16)


def solution(mesh):
    in_specs = (
        P("groups", None),
        P("groups", "heads", "pool", None),
        P("groups", "heads", "pool", None),
        P(None, "groups", "pool"),
        P(None, "groups"),
        P("groups"),
        P("pool", "heads"),
        P("pool", "heads"),
        P("pool", "heads"),
        P("heads", "pool"),
        P(None, ("pool", "heads")),
        P(None, ("pool", "heads")),
        P(("pool", "heads"), None),
    )
    out_specs = P("groups", "pool")
    return jax.shard_map(
        per_device, mesh=mesh, in_specs=in_specs, out_specs=out_specs, check_vma=False
    )
```

profile of v0, /device:TPU:1, one launch (start us, length us, event | category | flops | bytes accessed | tf_op | source)
XLA Modules:
  0.0 357.3 jit_solution(8407712216756091066)
XLA Ops:
  6.5 1.1 convert_element_type.78
  7.6 1.1 multiply_reduce_fusion
  8.8 0.3 fusion.54
  9.1 1.5 fusion.50
  10.6 4.6 %fusion.52 = f32[16,4096]{1,0:T(8,128)S(1)} fusion(bf16[1024,4096]{1,0:T(8,128)(2,1)} %param.19, f32[16,8192]{1,0:T(8,128)S(1)} %convert_element_type.78, s32[]{:T(128)S(6)} %select_n.82, f32[16]{0:T(128)S(1)} %add_rsqrt_fusion.1), kind=kOutput, calls=%fused_computation.96 | convolution fusion | flops 134250496 | bytes 8716804 | tf_op jit(solution)/shard_map/dot_general | solution.py:125
  15.2 0.1 concatenate.27
  15.3 0.7 pad_maximum_fusion
  16.1 11.3 %convert_element_type.82 = f32[16,4,512,128]{3,2,1,0:T(8,128)} convert(bf16[16,4,512,128]{3,2,1,0:T(8,128)(2,1)} %param.14) | non-fusion elementwise | flops 4194304 | bytes 25165824 | tf_op jit(solution)/shard_map/convert_element_type | solution.py:138
  27.5 0.1 copy.22
  27.6 0.6 gather_fusion
  28.2 0.2 slice_reduce_fusion.2
  28.4 0.1 broadcast_in_dim.119
  28.5 0.1 lt.54
  28.5 42.2 %fusion.5 = (f32[16,512,64]{2,1,0:T(8,128)S(1)}, f32[16,512,64]{2,1,0:T(8,128)S(1)}) fusion(f32[64]{0:T(128)S(1)} %multiply_exponential_fusion, s32[16,512]{1,0:T(8,128)S(1)} %get-tuple-element.23, s32[16,512]{1,0:T(8,128)S(1)} %get-tuple-element.24, s32[16,512]{1,0:T(8,128)S(1)} %get-tuple-element.22, pred[64]{0:T(512)(128)(4,1)S(1)} %get-tuple-element.29, ...), kind=kLoop, calls=%fused_computation.9 | loop fusion | flops 2097152 | bytes 4292992 | tf_op jit(solution)/shard_map/cos | solution.py:31
  70.7 19.2 %subtract_convert_fusion = (bf16[16,4,512,64]{3,2,1,0:T(8,128)(2,1)}, bf16[16,4,512,64]{3,2,1,0:T(8,128)(2,1)}) fusion(f32[16,4,512,128]{3,2,1,0:T(8,128)} %convert_element_type.82, f32[16,512,64]{2,1,0:T(8,128)S(1)} %get-tuple-element.21, f32[16,512,64]{2,1,0:T(8,128)S(1)} %get-tuple-element.20), kind=kLoop, calls=%fused_computation.2 | loop fusion | flops 16777216 | bytes 29360128 | tf_op jit(solution)/shard_map/convert.6
  90.0 0.1 broadcast_compare_fusion
  90.1 1.0 slice_bitcast_fusion
  91.1 1.1 subtract_convert_fusion.2
  92.2 0.2 subtract_convert_fusion.1
  92.4 9.3 %fusion.49 = (f32[64,8]{1,0:T(8,128)}, f32[64,8,512]{2,1,0:T(8,128)S(1)}) fusion(bf16[64,512,64]{2,1,0:T(8,128)(2,1)} %bitcast.54, bf16[64,512,64]{2,1,0:T(8,128)(2,1)} %bitcast.53, bf16[64,8,64]{2,1,0:T(8,128)(2,1)S(1)} %get-tuple-element.19, bf16[64,8,64]{2,1,0:T(8,128)(2,1)S(1)} %get-tuple-element.18, pred[64,512]{1,0:T(8,128)(4,1)S(1)} %broadcast_compare_fusion), kind=kOutput, calls=%fused_computation.94 | convolution fusion | flops 84934144 | bytes 9603072 | tf_op jit(solution)/shard_map/igd,isd->igs/dot_general | solution.py:67
  101.6 6.3 %all-to-all-start.1 = ((f32[64,1,8]{2,1,0:T(1,128)}), f32[64,1,8]{2,1,0:T(1,128)S(1)}, u32[]{:S(2)}, u32[]{:S(2)}) async-start(f32[64,1,8]{2,1,0:T(1,128)} %bitcast.11), calls=%async_computation.1 | async-start | bytes 65536 | tf_op jit(solution)/shard_map/all_to_all | solution.py:152
  108.0 0.1 fusion.41
  108.0 0.2 fusion.36
  108.2 5.4 %fusion.14 = f32[64,8,128]{2,1,0:T(8,128)} fusion(bf16[64,512,128]{2,1,0:T(8,128)(2,1)} %bitcast.55, f32[64,8,512]{2,1,0:T(8,128)S(1)} %get-tuple-element.28, f32[64,8]{1,0:T(8,128)} %get-tuple-element.27, pred[64,512]{1,0:T(8,128)(4,1)S(1)} %broadcast_compare_fusion), kind=kOutput, calls=%fused_computation.16 | convolution fusion | flops 67633152 | bytes 9734144 | tf_op jit(solution)/shard_map/igs,isd->igd/dot_general | solution.py:75
  113.6 1.7 fusion.13
  115.3 0.8 slice.72
  116.1 5.4 %all-to-all-start.2 = ((f32[64,1,8]{2,1,0:T(1,128)}), f32[64,1,8]{2,1,0:T(1,128)S(1)}, u32[]{:S(2)}, u32[]{:S(2)}) async-start(f32[64,1,8]{2,1,0:T(1,128)} %bitcast.21), calls=%async_computation.2 | async-start | bytes 65536 | tf_op jit(solution)/shard_map/all_to_all | solution.py:153
  121.6 5.5 %all-to-all-done.2 = f32[64,1,8]{2,1,0:T(1,128)S(1)} async-done(((f32[64,1,8]{2,1,0:T(1,128)}), f32[64,1,8]{2,1,0:T(1,128)S(1)}, u32[]{:S(2)}, u32[]{:S(2)}) %all-to-all-start.2) | async-done | bytes 2080 | tf_op jit(solution)/shard_map/all_to_all | solution.py:153
  127.1 3.4 all-to-all-start
  130.5 0.0 all-reduce.6.cloned.1.call-start
  130.6 0.1 copy.25
  130.7 0.1 copy.24
  130.7 6.9 %all-to-all-done = f32[64,1,1024]{2,1,0:T(1,128)S(1)} async-done(((f32[64,1,1024]{2,1,0:T(1,128)}), f32[64,1,1024]{2,1,0:T(1,128)S(1)}, u32[]{:S(2)}, u32[]{:S(2)}) %all-to-all-start) | async-done | bytes 262176 | tf_op jit(solution)/shard_map/all_to_all | solution.py:154
  137.6 0.1 mul.222
  137.7 0.4 multiply_reduce_fusion.1
  138.1 0.1 fusion.31
  138.2 24.3 %all_gather.6 = bf16[64,1024]{1,0:T(8,128)(2,1)S(1)} all-gather(bf16[8,1024]{1,0:T(8,128)(2,1)S(1)} %fusion.31), channel_id=1, replica_groups=mesh['groups'=2,'pool'=8,'heads'=2] {'pool'}, dimensions={0}, use_global_device_ids=true | all-gather | bytes 147456 | tf_op jit(solution)/shard_map/all_gather | solution.py:163
  162.5 0.1 reshape.304
  162.6 5.2 %fusion.56 = f32[16,1024]{1,0:T(8,128)} fusion(bf16[16,4096]{1,0:T(8,128)(2,1)S(1)} %reshape.304, bf16[4096,1024]{1,0:T(8,128)(2,1)} %param.22), kind=kOutput, calls=%fused_computation.98 | convolution fusion | flops 134217728 | bytes 8585216 | tf_op jit(solution)/shard_map/dot_general | solution.py:166
  167.9 25.8 %all-reduce.6.cloned.1.call-done = f32[16,1024]{1,0:T(8,128)} async-done(((f32[16,1024]{1,0:T(8,128)}), f32[16,1024]{1,0:T(8,128)}) %all-reduce.6.cloned.1.call-update) | async-done | bytes 65552 | tf_op jit(solution)/shard_map/psum | solution.py:166
  193.7 1.0 fusion.23
  194.6 24.7 %all_gather.7 = bf16[16,8192]{1,0:T(8,128)(2,1)S(1)} all-gather(bf16[16,1024]{1,0:T(8,128)(2,1)S(1)} %get-tuple-element.9), channel_id=1, replica_groups=mesh['groups'=2,'pool'=8,'heads'=2] {'pool'}, dimensions={1}, use_global_device_ids=true | all-gather | bytes 294912 | tf_op jit(solution)/shard_map/all_gather | solution.py:170
  219.4 17.5 %psum.30 = f32[16]{0:T(128)S(1)} all-reduce(f32[16]{0:T(128)S(1)} %get-tuple-element.8), channel_id=1, replica_groups=mesh['groups'=2,'pool'=8,'heads'=2] {'pool'}, use_global_device_ids=true, to_apply=%region_9.10 | all-reduce | flops 16 | bytes 128 | tf_op jit(solution)/shard_map/psum | solution.py:169
  236.9 9.4 %fusion.22 = f32[16,928]{1,0:T(8,128)S(1)} fusion(bf16[8192,928]{0,1:T(8,128)(2,1)} %param.23, bf16[16,8192]{1,0:T(8,128)(2,1)S(1)} %all_gather.7, f32[16]{0:T(128)S(1)} %add_rsqrt_fusion), kind=kOutput, calls=%fused_computation.33 | convolution fusion | flops 243662848 | bytes 15525952 | tf_op jit(solution)/shard_map/dot_general | solution.py:173
  246.3 13.9 %fusion.15 = f32[16,8192]{1,0:T(8,128)} fusion(bf16[928,8192]{1,0:T(8,128)(2,1)} %param.25, bf16[8192,928]{0,1:T(8,128)(2,1)} %param.24, bf16[16,8192]{1,0:T(8,128)(2,1)S(1)} %all_gather.7, f32[16]{0:T(128)S(1)} %add_rsqrt_fusion, f32[16,928]{1,0:T(8,128)S(1)} %fusion.22), kind=kOutput, calls=%fused_computation.17 | convolution fusion | flops 487021568 | bytes 31254592 | tf_op jit(solution)/shard_map/dot_general | solution.py:176
  260.3 67.8 %reduce-scatter.2.cloned.1.call-done = f32[16,1024]{1,0:T(8,128)} async-done(((f32[16,8192]{1,0:T(8,128)}), f32[16,1024]{1,0:T(8,128)}) %reduce-scatter.2.cloned.1.call-update) | async-done | bytes 65552 | tf_op jit(solution)/shard_map/reduce_scatter | solution.py:177
  328.1 21.2 %all-reduce.8.cloned.1.call-done = f32[16,1024]{1,0:T(8,128)} async-done(((f32[16,1024]{1,0:T(8,128)}), f32[16,1024]{1,0:T(8,128)}) %all-reduce.8.cloned.1.call-update) | async-done | bytes 65552 | tf_op jit(solution)/shard_map/psum | solution.py:178
  349.3 1.5 fusion.24
  (35 shorter events, 0.4 us)
Async XLA Ops:
  6.5 2.2 copy-start
  6.5 83.6 %all-reduce.4.cloned.1.call-start = ((), (), s32[]{:S(2)}) async-start(), calls=%async_computation.4 | async-start | bytes 655360 | tf_op jit(solution)/shard_map/psum | solution.py:144
  16.1 11.4 %copy-start.2 = (s32[3,16,512]{2,1,0:T(8,128)S(1)}, s32[3,16,512]{2,1,0:T(8,128)}, u32[]{:S(2)}) copy-start(s32[3,16,512]{2,1,0:T(8,128)} %param.16) | copy-start | bytes 294916
  16.1 11.4 %copy-start.3 = (s32[3,16]{1,0:T(4,128)S(1)}, s32[3,16]{1,0:T(4,128)}, u32[]{:S(2)}) copy-start(s32[3,16]{1,0:T(4,128)} %param.17) | copy-start | bytes 580
  16.1 12.2 %copy-start.4 = (s32[16]{0:T(128)S(1)}, s32[16]{0:T(128)}, u32[]{:S(2)}) copy-start(s32[16]{0:T(128)} %param.18) | copy-start | bytes 196
  101.6 14.5 %all-to-all-start.1 = ((f32[64,1,8]{2,1,0:T(1,128)}), f32[64,1,8]{2,1,0:T(1,128)S(1)}, u32[]{:S(2)}, u32[]{:S(2)}) async-start(f32[64,1,8]{2,1,0:T(1,128)} %bitcast.11), calls=%async_computation.1 | async-start | bytes 65536 | tf_op jit(solution)/shard_map/all_to_all | solution.py:152
  116.1 11.0 %all-to-all-start.2 = ((f32[64,1,8]{2,1,0:T(1,128)}), f32[64,1,8]{2,1,0:T(1,128)S(1)}, u32[]{:S(2)}, u32[]{:S(2)}) async-start(f32[64,1,8]{2,1,0:T(1,128)} %bitcast.21), calls=%async_computation.2 | async-start | bytes 65536 | tf_op jit(solution)/shard_map/all_to_all | solution.py:153
  127.1 10.5 %all-to-all-start = ((f32[64,1,1024]{2,1,0:T(1,128)}), f32[64,1,1024]{2,1,0:T(1,128)S(1)}, u32[]{:S(2)}, u32[]{:S(2)}) async-start(f32[64,1,1024]{2,1,0:T(1,128)} %bitcast.8), calls=%async_computation | async-start | bytes 524288 | tf_op jit(solution)/shard_map/all_to_all | solution.py:154
  130.5 63.2 %all-reduce.6.cloned.1.call-start = ((), (), s32[]{:S(2)}) async-start(), calls=%async_computation.5 | async-start | bytes 131072 | tf_op jit(solution)/shard_map/psum | solution.py:166
  167.9 160.3 %reduce-scatter.2.cloned.1.call-start = ((), (), s32[]{:S(2)}) async-start(), calls=%async_computation.6 | async-start | bytes 589824 | tf_op jit(solution)/shard_map/reduce_scatter | solution.py:177
  236.9 113.9 %copy-start.1 = (bf16[1024,512]{1,0:T(8,128)(2,1)S(1)}, bf16[1024,512]{1,0:T(8,128)(2,1)}, u32[]{:S(2)}) copy-start(bf16[1024,512]{1,0:T(8,128)(2,1)} %param.21) | copy-start | bytes 3145732
  260.3 89.0 %all-reduce.8.cloned.1.call-start = ((), (), s32[]{:S(2)}) async-start(), calls=%async_computation.7 | async-start | bytes 131072 | tf_op jit(solution)/shard_map/psum | solution.py:178
Sparse Core Ops, SparseCore 0:
  16.2 71.6 all-reduce.3
  168.0 25.6 all-reduce.5
  260.4 67.6 reduce-scatter.1
  330.3 19.0 all-reduce.7
where the time goes:
time: 358 us; the launch traced here: 357 us
  waiting for transfers between devices  127 us (35%)
  other arithmetic  81.8 us (23%)
  blocking collectives  66.6 us (19%)
  matrix products  49.8 us (14%)
  starting transfers between devices  15.3 us (4%)
  between operations  13.3 us (4%)
    reduce_scatter x1, waiting for transfers between devices, per_device(): lax.psum_scatter(partial_out, 'pool', scatter_dimension=1, tiled=True)  67.8 us
    cos x1, other arithmetic, angle_tables(): return (jnp.cos(angles), jnp.sin(angles))  42.2 us
    psum x1, waiting for transfers between devices, per_device(): lax.psum(jnp.dot(gathered, out_weight, preferred_element_type=jnp.float32...  25.8 us
    all_gather x1, blocking collectives, per_device(): whole_state = lax.all_gather(mid_state, 'pool', axis=1, tiled=True)  24.7 us
    all_gather x1, blocking collectives, per_device(): lax.all_gather(attended, 'pool', axis=0, tiled=True)  24.3 us
    psum x1, waiting for transfers between devices, per_device(): mlp_cols = lax.psum(mlp_cols, 'heads')  21.2 us
    another operation x3, other arithmetic  20.5 us
    psum x1, blocking collectives, per_device(): lax.psum(jnp.sum(jnp.square(mid_state.astype(jnp.float32)), -1), 'pool')  17.5 us
  transfers between devices with their start and end apart: 7, of which 5 were waited for; matrix products, arithmetic and copies ran while one was open for 23% of the time, Pallas kernels for 0%

commit v1 on v0

v1 whole, which is shorter than its diff:
```python
import functools
import math

import jax
import jax.numpy as jnp
from jax import lax
from jax.experimental import pallas as pl
from jax.experimental.pallas import tpu as pltpu
from jax.sharding import PartitionSpec as P

HD = 128
EPS = 1e-06
THETA = 1000000.0
MESH = pl.DeviceIdType.MESH
F32 = jnp.float32
BF16 = jnp.bfloat16

TURN_A = 6.28125
TURN_B = round((2 * math.pi - TURN_A) * 2**20) / 2**20
TURN_C = 2 * math.pi - TURN_A - TURN_B
SINE = [(-1) ** i / math.factorial(2 * i + 1) for i in range(7)]


def rope_tables(ids, inverse, lane):
    angle = ids * inverse
    upper = lane >= HD // 2
    quarter = jnp.where(upper, 0.25, 0.0).astype(F32)
    turns = jnp.floor(angle * (1.0 / (2 * math.pi)) - quarter + 0.5)
    rest = angle - turns * TURN_A
    rest = rest - turns * TURN_B
    rest = rest - turns * TURN_C
    half = (rest - quarter * (2 * math.pi)) * 0.5
    square = half * half
    poly = jnp.full_like(square, SINE[6])
    for i in range(5, -1, -1):
        poly = poly * square + SINE[i]
    sine = poly * half
    table = 1.0 - 2.0 * sine * sine
    swapped = pltpu.roll(table, HD // 2, 1)
    cos_table = jnp.where(upper, swapped, table)
    sin_table = jnp.where(upper, table, -swapped)
    return cos_table, sin_table


def make_kernel(n, prompts, lh, seq, d_model, ffl, group, wb, nslots, vslots, share):
    cb = d_model // n
    items = prompts * lh
    ipd = items // n
    per_head = prompts // ipd
    qw = group * HD
    cols = group + 2
    half_rows = prompts // 2
    nblocks = d_model // wb
    scale = HD ** (-0.5)

    def kernel(
        hidden, posx, sel, qsel, inv, lens, key_hbm, val_hbm, wq, wk, wv, wo, wg, wu, wd,
        out_ref,
        kbuf, vbuf, qkvbuf, wobuf, wgbuf, wubuf, chunk, chunk_in, tr, qg, acc, acc_in, ml, ml_in,
        atf, ats, atg, part, part_in, midf, mid_send, mg, ns, dpart, dother, ssum, rsum, yb, tabs,
        wsem, ksem, vsem, bigsem, dsem,
        s1, r1, s2, r2, s3, r3, s4, r4, s5, r5, s6, r6, s7, r7, s8, r8, hs, hr,
        *maybe_down,
    ):
        me = lax.axis_index("pool")
        hd = lax.axis_index("heads")
        other = 1 - hd

        def block_slot(b):
            buf = qkvbuf if share else maybe_down[0]
            slot = lax.rem(b, nslots)
            return buf.at[slot, pl.ds(0, ffl)] if share else buf.at[slot]

        def down_copy(b):
            return pltpu.make_async_copy(
                wd.at[:, pl.ds(pl.multiple_of(b * wb, wb), wb)], block_slot(b), dsem.at[lax.rem(b, nslots)]
            )

        def q_copy(h):
            return pltpu.make_async_copy(
                wq.at[:, pl.ds(pl.multiple_of(h * qw, qw), qw)], qkvbuf.at[h, pl.ds(0, cb)], wsem.at[h]
            )

        kv_copies = [
            pltpu.make_async_copy(wk, qkvbuf.at[0, pl.ds(0, cb), pl.ds(0, lh * HD)], wsem.at[lh]),
            pltpu.make_async_copy(wv, qkvbuf.at[0, pl.ds(0, cb), pl.ds(lh * HD, lh * HD)], wsem.at[lh + 1]),
        ]

        def k_copy(p):
            return pltpu.make_async_copy(key_hbm.at[p], kbuf.at[p], ksem.at[p])

        def v_copy(p):
            slot = lax.rem(p, vslots)
            return pltpu.make_async_copy(val_hbm.at[p], vbuf.at[slot], vsem.at[slot])

        wo_copy = pltpu.make_async_copy(wo, wobuf, bigsem.at[0])
        wg_copy = pltpu.make_async_copy(wg, wgbuf, bigsem.at[1])
        wu_copy = pltpu.make_async_copy(wu, wubuf, bigsem.at[2])

        for h in range(lh):
            q_copy(h).start()

        @pl.loop(0, prompts)
        def _(p):
            k_copy(p).start()

        for p in range(vslots):
            v_copy(p).start()
        wo_copy.start()
        wg_copy.start()
        wu_copy.start()

        barrier = pltpu.get_barrier_semaphore()

        @pl.loop(1, n)
        def _(k):
            pl.semaphore_signal(barrier, inc=1, device_id={"pool": lax.rem(me + k, n)}, device_id_type=MESH)

        pl.semaphore_signal(barrier, inc=1, device_id={"heads": other}, device_id_type=MESH)

        def pool_copy(src, dst, ssem, rsem, d):
            return pltpu.make_async_remote_copy(
                src_ref=src, dst_ref=dst, send_sem=ssem.at[d], recv_sem=rsem.at[me],
                device_id={"pool": d}, device_id_type=MESH,
            )

        def wait_from(src, dst, ssem, rsem, s):
            pltpu.make_async_remote_copy(
                src_ref=src, dst_ref=dst, send_sem=ssem.at[s], recv_sem=rsem.at[s],
                device_id={"pool": s}, device_id_type=MESH,
            ).wait_recv()

        def peers(body):
            @pl.loop(1, n)
            def _(k):
                body(lax.rem(me + k, n))

        lane_row = lax.broadcasted_iota(jnp.int32, (1, HD), 1)
        hid = hidden[...].astype(F32)
        inv_rms = lax.rsqrt(jnp.sum(hid * hid, -1, keepdims=True) * (1.0 / d_model) + EPS)
        my_cols = hidden[:, pl.ds(pl.multiple_of(me * cb, cb), cb)].astype(F32)
        normed = (my_cols * inv_rms).astype(BF16)

        def put(h, c, value):
            for t in range(per_head):
                chunk[h * per_head + t, c] = value[t * ipd : (t + 1) * ipd]

        @pl.loop(0, lh)
        def _(h):
            q_copy(h).wait()
            res = jnp.dot(normed, qkvbuf[h, 0:cb, :], preferred_element_type=F32)
            for c in range(group):
                put(h, c, res[:, c * HD : (c + 1) * HD])

            @pl.when(h == 0)
            def _():
                for c in kv_copies:
                    c.start()

        for c in kv_copies:
            c.wait()
        res = jnp.dot(normed, qkvbuf[0, 0:cb, :], preferred_element_type=F32)
        for h in range(lh):
            put(h, group, res[:, h * HD : (h + 1) * HD])
            put(h, group + 1, res[:, (lh + h) * HD : (lh + h + 1) * HD])

        for b in range(min(nslots, nblocks)):
            down_copy(b).start()

        pl.semaphore_wait(barrier, n)
        peers(lambda d: pool_copy(chunk.at[d], chunk_in.at[me], s1, r1, d).start())

        inv_row = inv[...]

        cos_q, sin_q = rope_tables(qsel[...], inv_row, lane_row)
        tabs[0] = cos_q
        tabs[1] = sin_q

        @pl.loop(0, prompts)
        def _(p):
            k_copy(p).wait()
            ids = lax.dot_general(posx[p], sel[...], (((0,), (0,)), ((), ())), preferred_element_type=F32)
            cos_table, sin_table = rope_tables(ids, inv_row, lane_row)
            for h in range(lh):
                keys = kbuf[p, h].astype(F32)
                swapped = pltpu.roll(keys, HD // 2, 1)
                kbuf[p, h] = (keys * cos_table + swapped * sin_table).astype(BF16)

        total = chunk[me]

        def add_in(k, total):
            s = lax.rem(me + k, n)
            wait_from(chunk.at[s], chunk_in.at[s], s1, r1, s)
            return total + chunk_in[s]

        total = lax.fori_loop(1, n, add_in, total)
        first_prompt = lax.rem(me * ipd, prompts)
        if ipd % 8 == 0:
            first_prompt = pl.multiple_of(first_prompt, 8)
        cos_mine = tabs[0, pl.ds(first_prompt, ipd), :]
        sin_mine = tabs[1, pl.ds(first_prompt, ipd), :]
        for c in range(cols):
            value = total[c]
            if c <= group:
                value = value * cos_mine + pltpu.roll(value, HD // 2, 1) * sin_mine
            tr[:, c, :] = value
        for c in range(cols, 16):
            tr[:, c, :] = jnp.zeros((ipd, HD), F32)
        qg[me] = tr[...].astype(BF16)
        peers(lambda d: pool_copy(qg.at[me], qg.at[me], s2, r2, d).start())
        peers(lambda s: wait_from(qg.at[me], qg.at[s], s2, r2, s))

        slot_index = lax.broadcasted_iota(jnp.int32, (1, seq), 1) + me * seq

        @pl.loop(0, prompts)
        def _(p):
            v_copy(p).wait()
            slot = lax.rem(p, vslots)
            valid = slot_index < lens[p]
            for h in range(lh):
                it = h * prompts + p
                d = it // ipd
                i = lax.rem(it, ipd)
                queries = qg[d, i][0:group]
                scores = lax.dot_general(
                    queries, kbuf[p, h], (((1,), (1,)), ((), ())), preferred_element_type=F32
                ) * scale
                scores = jnp.where(valid, scores, -1e30)
                peak = jnp.max(scores, -1, keepdims=True)
                weights = jnp.where(valid, jnp.exp(scores - peak), 0.0)
                sums = jnp.sum(weights, -1, keepdims=True)
                acc[d, i] = jnp.dot(weights.astype(BF16), vbuf[slot, h], preferred_element_type=F32)
                ml[d] = jnp.where(lane_row == i, peak, jnp.where(lane_row == i + HD // 2, sums, ml[d]))

            @pl.when(p + vslots < prompts)
            def _():
                v_copy(p + vslots).start()

        def send_partial(d):
            pool_copy(acc.at[d], acc_in.at[me], s3, r3, d).start()
            pool_copy(ml.at[d], ml_in.at[me], s4, r4, d).start()

        peers(send_partial)

        own_scores = []
        for i in range(ipd):
            row = qg[me, i].astype(F32)
            own_scores.append(jnp.sum(row[0:group] * row[group : group + 1], -1, keepdims=True) * scale)

        def wait_partial(s):
            wait_from(acc.at[s], acc_in.at[s], s3, r3, s)
            wait_from(ml.at[s], ml_in.at[s], s4, r4, s)

        peers(wait_partial)
        acc_in[me] = acc[me]
        ml_in[me] = ml[me]

        top_all = lax.fori_loop(0, n, lambda s, t: jnp.maximum(t, ml_in[s]), jnp.full((group, HD), -1e30, F32))
        for i in range(ipd):
            top = jnp.maximum(top_all[:, i : i + 1], own_scores[i])
            own_weight = jnp.exp(own_scores[i] - top)
            own_value = qg[me, i].astype(F32)[group + 1 : group + 2]

            def merge(s, carry):
                den, num = carry
                tile = ml_in[s]
                factor = jnp.exp(tile[:, i : i + 1] - top)
                return den + tile[:, HD // 2 + i : HD // 2 + i + 1] * factor, num + acc_in[s, i] * factor

            den, num = lax.fori_loop(
                0, n, merge, (own_weight, own_weight * own_value), unroll=n <= 8
            )
            atf[i] = num / den
        for j in range(group):
            ats[:, j * HD : (j + 1) * HD] = atf[:, j, :].astype(BF16)
        atg[me] = ats[...]
        peers(lambda d: pool_copy(ats, atg.at[me], s5, r5, d).start())
        peers(lambda s: wait_from(ats, atg.at[s], s5, r5, s))

        wo_copy.wait()
        part[...] = jnp.zeros_like(part)

        @pl.loop(0, lh)
        def _(h):
            rows = atg[pl.ds(h * per_head, per_head)].astype(F32).reshape(prompts, qw).astype(BF16)
            part[...] += jnp.dot(rows, wobuf[pl.ds(pl.multiple_of(h * qw, qw), qw), :], preferred_element_type=F32)

        def partner_copy(src, dst, idx):
            return pltpu.make_async_remote_copy(
                src_ref=src, dst_ref=dst, send_sem=hs.at[idx], recv_sem=hr.at[idx],
                device_id={"heads": other}, device_id_type=MESH,
            )

        part_copy = partner_copy(part, part_in, 0)
        part_copy.start()
        part_copy.wait_recv()
        mid = (my_cols + (part[...] + part_in[...])).astype(BF16).astype(F32)
        midf[0] = mid[0:half_rows]
        midf[1] = mid[half_rows:]
        mid_send[...] = midf[hd].astype(BF16)
        mg[hd, me] = mid_send[...]
        peers(lambda d: pool_copy(mid_send, mg.at[hd, me], s6, r6, d).start())
        peers(lambda s: wait_from(mid_send, mg.at[hd, s], s6, r6, s))
        half_copy = partner_copy(mg.at[hd], mg.at[hd], 1)
        half_copy.start()
        pltpu.make_async_remote_copy(
            src_ref=mg.at[other], dst_ref=mg.at[other], send_sem=hs.at[1], recv_sem=hr.at[1],
            device_id={"heads": other}, device_id_type=MESH,
        ).wait_recv()

        def squares(s, total):
            x = mg[:, s].astype(F32).reshape(prompts, cb)
            return total + jnp.sum(x * x, -1, keepdims=True)

        sq = lax.fori_loop(0, n, squares, jnp.zeros((prompts, 1), F32))
        inv_mid = lax.rsqrt(sq * (1.0 / d_model) + EPS)
        wg_copy.wait()
        wu_copy.wait()

        def ff(s, carry):
            g, u = carry
            x = (mg[:, s].astype(F32).reshape(prompts, cb) * inv_mid).astype(BF16)
            rows = pl.ds(pl.multiple_of(s * cb, cb), cb)
            g = g + jnp.dot(x, wgbuf[rows, :], preferred_element_type=F32)
            u = u + jnp.dot(x, wubuf[rows, :], preferred_element_type=F32)
            return g, u

        zero = jnp.zeros((prompts, ffl), F32)
        gate, up = lax.fori_loop(0, n, ff, (zero, zero))
        ns[...] = (gate / (1.0 + jnp.exp(-gate)) * up).astype(BF16)

        per_block = wb // cb

        def dother_copy(d):
            return pltpu.make_async_remote_copy(
                src_ref=dpart.at[other, d], dst_ref=dother.at[d], send_sem=s7.at[d], recv_sem=r7.at[d],
                device_id={"heads": other}, device_id_type=MESH,
            )

        @pl.loop(0, nblocks)
        def _(b):
            down_copy(b).wait()
            slot = lax.rem(b, nslots)
            w = qkvbuf[slot, 0:ffl, :] if share else maybe_down[0][slot]
            res = jnp.dot(ns[...], w, preferred_element_type=F32)
            for t in range(per_block):
                d = b * per_block + t
                dpart[0, d] = res[0:half_rows, t * cb : (t + 1) * cb]
                dpart[1, d] = res[half_rows:, t * cb : (t + 1) * cb]
                dother_copy(d).start()

            @pl.when(b + nslots < nblocks)
            def _():
                down_copy(b + nslots).start()

        def reduce_and_send(d):
            dother_copy(d).wait_recv()
            ssum[d] = dpart[hd, d] + dother[d]
            pool_copy(ssum.at[d], rsum.at[me], s8, r8, d).start()

        peers(reduce_and_send)
        dother_copy(me).wait_recv()
        final = dpart[hd, me] + dother[me]

        def add_final(k, total):
            s = lax.rem(me + k, n)
            wait_from(ssum.at[s], rsum.at[s], s8, r8, s)
            return total + rsum[s]

        final = lax.fori_loop(1, n, add_final, final)
        yb[hd] = (midf[hd] + final).astype(BF16)
        y_copy = partner_copy(yb.at[hd], yb.at[hd], 2)
        y_copy.start()
        pltpu.make_async_remote_copy(
            src_ref=yb.at[other], dst_ref=yb.at[other], send_sem=hs.at[2], recv_sem=hr.at[2],
            device_id={"heads": other}, device_id_type=MESH,
        ).wait_recv()
        out_ref[...] = yb[...].astype(F32).reshape(prompts, cb).astype(BF16)

        def drain(d):
            pool_copy(chunk.at[d], chunk_in.at[me], s1, r1, d).wait_send()
            pool_copy(qg.at[me], qg.at[me], s2, r2, d).wait_send()
            pool_copy(acc.at[d], acc_in.at[me], s3, r3, d).wait_send()
            pool_copy(ml.at[d], ml_in.at[me], s4, r4, d).wait_send()
            pool_copy(ats, atg.at[me], s5, r5, d).wait_send()
            pool_copy(mid_send, mg.at[hd, me], s6, r6, d).wait_send()
            pool_copy(ssum.at[d], rsum.at[me], s8, r8, d).wait_send()

        peers(drain)

        @pl.loop(0, n)
        def _(d):
            dother_copy(d).wait_send()

        part_copy.wait_send()
        half_copy.wait_send()
        y_copy.wait_send()

    return kernel


def per_device(
    n, hidden_in, key_cache, value_cache, positions, query_pos, lengths,
    query_weight, key_weight, value_weight, out_weight, gate_weight, up_weight, down_weight,
):
    prompts, d_model = hidden_in.shape
    lh, seq = key_cache.shape[1:3]
    cb = d_model // n
    ffl = gate_weight.shape[1]
    group = query_weight.shape[1] // key_weight.shape[1]
    qw = group * HD
    wb = max(cb, qw)
    nblocks = d_model // wb
    nslots = min(lh, nblocks)
    share = ffl % 16 == 0 and ffl <= cb and wb == qw
    vslots = 3
    items = prompts * lh
    ipd = items // n

    column = jnp.arange(HD) % (HD // 2)
    inverse = jnp.exp(column.astype(F32) * (-2.0 * math.log(THETA) / HD))[None]
    first_end = HD // 8
    second_end = first_end + 3 * HD // 16
    which = jnp.where(column < first_end, 0, jnp.where(column < second_end, 1, 2))
    hit = (which[None] == jnp.arange(3)[:, None]).astype(F32)
    pad = jnp.zeros((2, HD), F32)
    sel = jnp.concatenate([64.0 * hit, hit, pad], 0).astype(BF16)
    spread = jnp.transpose(positions, (1, 0, 2))
    posx = jnp.concatenate(
        [spread // 64, spread % 64, jnp.zeros((prompts, 2, seq), jnp.int32)], 1
    ).astype(BF16)
    qpos = query_pos.astype(F32)
    qsel = jnp.where(
        column < first_end, qpos[0][:, None], jnp.where(column < second_end, qpos[1][:, None], qpos[2][:, None])
    )

    kernel = make_kernel(n, prompts, lh, seq, d_model, ffl, group, wb, nslots, vslots, share)
    half = prompts // 2
    vm = pltpu.VMEM
    dma = pltpu.SemaphoreType.DMA
    scratch = [
        vm((prompts, lh, seq, HD), BF16),
        vm((vslots, lh, seq, HD), BF16),
        vm((lh, cb, qw), BF16),
        vm(out_weight.shape, BF16),
        vm(gate_weight.shape, BF16),
        vm(up_weight.shape, BF16),
        vm((n, group + 2, ipd, HD), F32),
        vm((n, group + 2, ipd, HD), F32),
        vm((ipd, 16, HD), F32),
        vm((n, ipd, 16, HD), BF16),
        vm((n, ipd, group, HD), F32),
        vm((n, ipd, group, HD), F32),
        vm((n, group, HD), F32),
        vm((n, group, HD), F32),
        vm((ipd, group, HD), F32),
        vm((ipd, qw), BF16),
        vm((n, ipd, qw), BF16),
        vm((prompts, cb), F32),
        vm((prompts, cb), F32),
        vm((2, half, cb), F32),
        vm((half, cb), BF16),
        vm((2, n, half, cb), BF16),
        vm((prompts, ffl), BF16),
        vm((2, n, half, cb), F32),
        vm((n, half, cb), F32),
        vm((n, half, cb), F32),
        vm((n, half, cb), F32),
        vm((2, half, cb), BF16),
        vm((2, prompts, HD), F32),
        dma((lh + 2,)),
        dma((prompts,)),
        dma((vslots,)),
        dma((3,)),
        dma((nslots,)),
    ] + [dma((n,)) for _ in range(16)] + [dma((3,)), dma((3,))]
    if not share:
        scratch.append(vm((nslots, ffl, wb), BF16))
    in_vmem = pl.BlockSpec(memory_space=pltpu.VMEM)
    in_any = pl.BlockSpec(memory_space=pl.ANY)
    return pl.pallas_call(
        kernel,
        out_shape=jax.ShapeDtypeStruct((prompts, cb), BF16),
        in_specs=[in_vmem] * 5 + [pl.BlockSpec(memory_space=pltpu.SMEM)] + [in_any] * 9,
        out_specs=in_vmem,
        scratch_shapes=scratch,
        compiler_params=pltpu.CompilerParams(
            collective_id=0, has_side_effects=True, vmem_limit_bytes=67043328
        ),
    )(
        hidden_in, posx, sel, qsel, inverse, lengths, key_cache, value_cache,
        query_weight, key_weight, value_weight, out_weight, gate_weight, up_weight, down_weight,
    )


def solution(mesh):
    in_specs = (
        P("groups", None),
        P("groups", "heads", "pool", None),
        P("groups", "heads", "pool", None),
        P(None, "groups", "pool"),
        P(None, "groups"),
        P("groups"),
        P("pool", "heads"),
        P("pool", "heads"),
        P("pool", "heads"),
        P("heads", "pool"),
        P(None, ("pool", "heads")),
        P(None, ("pool", "heads")),
        P(("pool", "heads"), None),
    )
    return jax.shard_map(
        functools.partial(per_device, mesh.shape["pool"]),
        mesh=mesh,
        in_specs=in_specs,
        out_specs=P("groups", "pool"),
        check_vma=False,
    )
```

time: 358 us -> 150 us (0.42)
  waiting for transfers between devices: 127 us -> 0 us
  Pallas kernels: 0 us -> 99.5 us
  other arithmetic: 81.8 us -> 4.45 us
  blocking collectives: 66.6 us -> 0 us
  matrix products: 49.8 us -> 0 us
  local copies, waits for them, and re-layouts: 3.27 us -> 45.2 us
  starting transfers between devices: 15.3 us -> 0 us
  between operations: 13.3 us -> 0.02 us
    pallas_call x0 -> x1, Pallas kernels: none -> 99.5 us  [per_device(): pl.pallas_call(kernel, out_shape=jax.ShapeDtypeStruct((prompts, cb), BF16...]
    reduce_scatter x1 -> x0, waiting for transfers between devices: 67.8 us -> none  [per_device(): lax.psum_scatter(partial_out, 'pool', scatter_dimension=1, tiled=True)]
    dot_general x9 -> x0, matrix products: 49.8 us -> none  [the longest x1 13.9 us: per_device(): jnp.dot(active, down_weight, preferred_element_type=jnp.float32)]
    all_gather x2 -> x0, blocking collectives: 49.1 us -> none  [the longest x1 24.7 us: per_device(): whole_state = lax.all_gather(mid_state, 'pool', axis=1, tiled=True)]
    psum x3 -> x0, waiting for transfers between devices: 47 us -> none  [the longest x1 25.8 us: per_device(): lax.psum(jnp.dot(gathered, out_weight, preferred_element_type=jnp.float32...]
    unnamed x13 -> x3, local copies, waits for them, and re-layouts: 1.13 us -> 45.1 us
    cos x1 -> x0, other arithmetic: 42.2 us -> none  [angle_tables(): return (jnp.cos(angles), jnp.sin(angles))]
    another operation x3, other arithmetic: 20.5 us -> 1.18 us
  transfers between devices with their start and end apart: 7 -> 0, of which waited for: 5 -> 0; matrix products, arithmetic and copies ran while one was open for 23% -> 0% of each run, Pallas kernels for 0% -> 0%
where the time goes in v1:
time: 150 us; the launch traced here: 149 us
  Pallas kernels  99.5 us (66%)
  local copies, waits for them, and re-layouts  45.2 us (30%)
  other arithmetic  4.45 us (3%)
    pallas_call x1, Pallas kernels, per_device(): pl.pallas_call(kernel, out_shape=jax.ShapeDtypeStruct((prompts, cb), BF16...  99.5 us
    unnamed x3, local copies, waits for them, and re-layouts  45.1 us

profile of v1, /device:TPU:1, one launch (start us, length us, event | category | flops | bytes accessed | tf_op | source)
XLA Modules:
  0.0 149.1 jit_solution(4587459673884441404)
XLA Ops:
  0.0 0.1 pad.5.clone
  0.1 0.5 fusion.6.inv
  0.6 0.6 maximum_maximum_fusion.1.sel
  1.3 0.7 convert_element_type.19
  1.9 0.7 select_select_fusion.qsel
  2.6 1.2 fusion
  3.8 0.8 maximum_maximum_fusion.posx
  4.5 21.9 %copy.15.wg = bf16[8192,928]{1,0:T(8,128)(2,1)} copy(bf16[8192,928]{0,1:T(8,128)(2,1)} %param.23) | data formatting | bytes 30408704 | tf_op args[10]
  26.4 21.8 %copy.16.wu = bf16[8192,928]{1,0:T(8,128)(2,1)} copy(bf16[8192,928]{0,1:T(8,128)(2,1)} %param.24) | data formatting | bytes 30408704 | tf_op args[11]
  48.3 99.5 %shard_map.127 = bf16[16,1024]{1,0:T(8,128)(2,1)} custom-call(bf16[16,8192]{1,0:T(8,128)(2,1)} %hidden.1, bf16[16,8,512]{2,1,0:T(8,128)(2,1)} %maximum_maximum_fusion.posx, bf16[8,128]{1,0:T(8,128)(2,1)} %maximum_maximum_fusion.1.sel, f32[16,128]{1,0:T(8,128)} %select_select_fusion.qsel, f32[1,128]{1,0:T(1,128)} %fusion.6.inv, s32[16]{0:T(128)} %lens.1, ...), custom_call_target="tpu_custom_call" | custom-call | tf_op jit(solution)/shard_map/pallas_call | solution.py:481
  147.7 1.4 copy.39
  (6 shorter events, 0.0 us)

commit v2 on v1

--- a/solution.py
+++ b/solution.py
@@ -321,8 +321,9 @@
             g, u = carry
             x = (mg[:, s].astype(F32).reshape(prompts, cb) * inv_mid).astype(BF16)
             rows = pl.ds(pl.multiple_of(s * cb, cb), cb)
-            g = g + jnp.dot(x, wgbuf[rows, :], preferred_element_type=F32)
-            u = u + jnp.dot(x, wubuf[rows, :], preferred_element_type=F32)
+            nt = (((1,), (1,)), ((), ()))
+            g = g + lax.dot_general(x, wgbuf[:, rows], nt, preferred_element_type=F32)
+            u = u + lax.dot_general(x, wubuf[:, rows], nt, preferred_element_type=F32)
             return g, u
 
         zero = jnp.zeros((prompts, ffl), F32)
@@ -443,8 +444,8 @@
         vm((vslots, lh, seq, HD), BF16),
         vm((lh, cb, qw), BF16),
         vm(out_weight.shape, BF16),
-        vm(gate_weight.shape, BF16),
-        vm(up_weight.shape, BF16),
+        vm((ffl, d_model), BF16),
+        vm((ffl, d_model), BF16),
         vm((n, group + 2, ipd, HD), F32),
         vm((n, group + 2, ipd, HD), F32),
         vm((ipd, 16, HD), F32),
@@ -489,7 +490,7 @@
         ),
     )(
         hidden_in, posx, sel, qsel, inverse, lengths, key_cache, value_cache,
-        query_weight, key_weight, value_weight, out_weight, gate_weight, up_weight, down_weight,
+        query_weight, key_weight, value_weight, out_weight, gate_weight.T, up_weight.T, down_weight,
     )
 
 

time: 150 us -> 108 us (0.72)
  local copies, waits for them, and re-layouts: 45.2 us -> 1.46 us
  Pallas kernels: 99.5 us -> 102 us
    unnamed x3 -> x1, local copies, waits for them, and re-layouts: 45.1 us -> 1.38 us
    pallas_call x1, Pallas kernels: 99.5 us -> 102 us  [per_device(): pl.pallas_call(kernel, out_shape=jax.ShapeDtypeStruct((prompts, cb), BF16...]
where the time goes in v2:
time: 108 us
  Pallas kernels  102 us (94%)
  other arithmetic  4.44 us (4%)
  local copies, waits for them, and re-layouts  1.46 us (1%)
    pallas_call x1, Pallas kernels, per_device(): pl.pallas_call(kernel, out_shape=jax.ShapeDtypeStruct((prompts, cb), BF16...  102 us

profile of v2, /device:TPU:1, one launch (start us, length us, event | category | flops | bytes accessed | tf_op | source)
XLA Modules:
  0.0 108.2 jit_solution(10937574104905236671)
XLA Ops:
  0.0 1.2 %fusion = (bf16[16,3,512]{2,1,0:T(4,128)(2,1)S(1)}, bf16[16,3,512]{2,1,0:T(4,128)(2,1)S(1)}) fusion(s32[3,16,512]{2,1,0:T(8,128)} %param.16), kind=kLoop, calls=%fused_computation.5 | loop fusion | flops 516096 | bytes 196608 | tf_op jit(solution)/shard_map/convert.3
  1.2 0.1 pad.5.clone
  1.3 0.7 maximum_maximum_fusion.posx
  2.0 0.6 maximum_maximum_fusion.1.sel
  2.7 0.7 convert_element_type.19
  3.4 0.7 select_select_fusion.qsel
  4.0 0.5 fusion.6.inv
  4.6 102.3 %shard_map.127 = bf16[16,1024]{1,0:T(8,128)(2,1)} custom-call(bf16[16,8192]{1,0:T(8,128)(2,1)} %hidden.1, bf16[16,8,512]{2,1,0:T(8,128)(2,1)} %maximum_maximum_fusion.posx, bf16[8,128]{1,0:T(8,128)(2,1)} %maximum_maximum_fusion.1.sel, f32[16,128]{1,0:T(8,128)} %select_select_fusion.qsel, f32[1,128]{1,0:T(1,128)} %fusion.6.inv, s32[16]{0:T(128)} %lens.1, ...), custom_call_target="tpu_custom_call" | custom-call | tf_op jit(solution)/shard_map/pallas_call | solution.py:482
  106.8 1.4 %copy.37 = bf16[16,1024]{1,0:T(8,128)(2,1)} copy(bf16[16,1024]{1,0:T(8,128)(2,1)} %shard_map.127) | data formatting | bytes 65536
  (6 shorter events, 0.0 us)

commit v3 on v2

--- a/solution.py
+++ b/solution.py
@@ -3,6 +3,7 @@
 
 import jax
 import jax.numpy as jnp
+import numpy as np
 from jax import lax
 from jax.experimental import pallas as pl
 from jax.experimental.pallas import tpu as pltpu
@@ -54,7 +55,7 @@
     scale = HD ** (-0.5)
 
     def kernel(
-        hidden, posx, sel, qsel, inv, lens, key_hbm, val_hbm, wq, wk, wv, wo, wg, wu, wd,
+        hidden, pos, qpos, sel, inv, lens, key_hbm, val_hbm, wq, wk, wv, wo, wg, wu, wd,
         out_ref,
         kbuf, vbuf, qkvbuf, wobuf, wgbuf, wubuf, chunk, chunk_in, tr, qg, acc, acc_in, ml, ml_in,
         atf, ats, atg, part, part_in, midf, mid_send, mg, ns, dpart, dother, ssum, rsum, yb, tabs,
@@ -89,9 +90,13 @@
         def k_copy(p):
             return pltpu.make_async_copy(key_hbm.at[p], kbuf.at[p], ksem.at[p])
 
-        def v_copy(p):
-            slot = lax.rem(p, vslots)
-            return pltpu.make_async_copy(val_hbm.at[p], vbuf.at[slot], vsem.at[slot])
+        def v_copy(k):
+            d = lax.rem(me + k, n)
+            slot = lax.rem(k, vslots)
+            first = pl.multiple_of(lax.rem(d, per_head) * ipd, ipd)
+            return pltpu.make_async_copy(
+                val_hbm.at[pl.ds(first, ipd), d // per_head], vbuf.at[slot], vsem.at[slot]
+            )
 
         wo_copy = pltpu.make_async_copy(wo, wobuf, bigsem.at[0])
         wg_copy = pltpu.make_async_copy(wg, wgbuf, bigsem.at[1])
@@ -104,8 +109,8 @@
         def _(p):
             k_copy(p).start()
 
-        for p in range(vslots):
-            v_copy(p).start()
+        for k in range(1, vslots + 1):
+            v_copy(k).start()
         wo_copy.start()
         wg_copy.start()
         wu_copy.start()
@@ -172,19 +177,28 @@
 
         inv_row = inv[...]
 
-        cos_q, sin_q = rope_tables(qsel[...], inv_row, lane_row)
+        def split(ids):
+            high = jnp.floor(ids * (1.0 / 64.0))
+            pad = jnp.zeros((2, ids.shape[1]), F32)
+            return jnp.concatenate([high, ids - 64.0 * high, pad], 0).astype(BF16)
+
+        def pick(ids):
+            return lax.dot_general(split(ids), sel[...], (((0,), (0,)), ((), ())), preferred_element_type=F32)
+
+        cos_q, sin_q = rope_tables(pick(qpos[...].astype(F32)), inv_row, lane_row)
         tabs[0] = cos_q
         tabs[1] = sin_q
 
-        @pl.loop(0, prompts)
-        def _(p):
+        def rotate_prompt(p):
             k_copy(p).wait()
-            ids = lax.dot_general(posx[p], sel[...], (((0,), (0,)), ((), ())), preferred_element_type=F32)
+            ids = pick(pos[:, p, :].astype(F32))
             cos_table, sin_table = rope_tables(ids, inv_row, lane_row)
             for h in range(lh):
                 keys = kbuf[p, h].astype(F32)
                 swapped = pltpu.roll(keys, HD // 2, 1)
                 kbuf[p, h] = (keys * cos_table + swapped * sin_table).astype(BF16)
+
+        pl.loop(0, prompts // 2)(rotate_prompt)
 
         total = chunk[me]
 
@@ -208,44 +222,63 @@
             tr[:, c, :] = jnp.zeros((ipd, HD), F32)
         qg[me] = tr[...].astype(BF16)
         peers(lambda d: pool_copy(qg.at[me], qg.at[me], s2, r2, d).start())
+        pl.loop(prompts // 2, prompts)(rotate_prompt)
         peers(lambda s: wait_from(qg.at[me], qg.at[s], s2, r2, s))
 
         slot_index = lax.broadcasted_iota(jnp.int32, (1, seq), 1) + me * seq
 
-        @pl.loop(0, prompts)
-        def _(p):
-            v_copy(p).wait()
-            slot = lax.rem(p, vslots)
-            valid = slot_index < lens[p]
-            for h in range(lh):
-                it = h * prompts + p
-                d = it // ipd
-                i = lax.rem(it, ipd)
-                queries = qg[d, i][0:group]
-                scores = lax.dot_general(
-                    queries, kbuf[p, h], (((1,), (1,)), ((), ())), preferred_element_type=F32
-                ) * scale
-                scores = jnp.where(valid, scores, -1e30)
-                peak = jnp.max(scores, -1, keepdims=True)
-                weights = jnp.where(valid, jnp.exp(scores - peak), 0.0)
+        batch = min(4, ipd)
+
+        @pl.loop(1, n + 1)
+        def _(k):
+            d = lax.rem(me + k, n)
+            v_copy(k).wait()
+            slot = lax.rem(k, vslots)
+            h = d // per_head
+            first = lax.rem(d, per_head) * ipd
+            tile = jnp.zeros((group, HD), F32)
+            for i0 in range(0, ipd, batch):
+                raw = []
+                for i in range(i0, i0 + batch):
+                    queries = qg[d, i][0:group]
+                    scores = lax.dot_general(
+                        queries, kbuf[first + i, h], (((1,), (1,)), ((), ())), preferred_element_type=F32
+                    ) * scale
+                    raw.append(jnp.where(slot_index < lens[first + i], scores, -1e30))
+                stacked = jnp.concatenate(raw, 0)
+                peak = jnp.maximum(jnp.max(stacked, -1, keepdims=True), -1e29)
+                weights = jnp.exp(stacked - peak)
                 sums = jnp.sum(weights, -1, keepdims=True)
-                acc[d, i] = jnp.dot(weights.astype(BF16), vbuf[slot, h], preferred_element_type=F32)
-                ml[d] = jnp.where(lane_row == i, peak, jnp.where(lane_row == i + HD // 2, sums, ml[d]))
-
-            @pl.when(p + vslots < prompts)
+                low = weights.astype(BF16)
+                blended = []
+                for j in range(batch):
+                    i = i0 + j
+                    rows = slice(j * group, (j + 1) * group)
+                    blended.append(
+                        jnp.dot(low[rows], vbuf[slot, i], preferred_element_type=F32)
+                    )
+                    tile = jnp.where(
+                        lane_row == i, peak[rows], jnp.where(lane_row == i + HD // 2, sums[rows], tile)
+                    )
+                acc[d, i0 * group : (i0 + batch) * group] = jnp.concatenate(blended, 0).astype(BF16)
+            ml[d] = tile
+
+            @pl.when(k < n)
             def _():
-                v_copy(p + vslots).start()
-
-        def send_partial(d):
-            pool_copy(acc.at[d], acc_in.at[me], s3, r3, d).start()
-            pool_copy(ml.at[d], ml_in.at[me], s4, r4, d).start()
-
-        peers(send_partial)
-
-        own_scores = []
+                pool_copy(acc.at[d], acc_in.at[me], s3, r3, d).start()
+                pool_copy(ml.at[d], ml_in.at[me], s4, r4, d).start()
+
+            @pl.when(k + vslots < n + 1)
+            def _():
+                v_copy(k + vslots).start()
+
+        own_tile = jnp.full((group, HD), -1e30, F32)
+        own_values = []
         for i in range(ipd):
             row = qg[me, i].astype(F32)
-            own_scores.append(jnp.sum(row[0:group] * row[group : group + 1], -1, keepdims=True) * scale)
+            own = jnp.sum(row[0:group] * row[group : group + 1], -1, keepdims=True) * scale
+            own_tile = jnp.where(lane_row == i, own, own_tile)
+            own_values.append(row[group + 1 : group + 2])
 
         def wait_partial(s):
             wait_from(acc.at[s], acc_in.at[s], s3, r3, s)
@@ -255,22 +288,25 @@
         acc_in[me] = acc[me]
         ml_in[me] = ml[me]
 
-        top_all = lax.fori_loop(0, n, lambda s, t: jnp.maximum(t, ml_in[s]), jnp.full((group, HD), -1e30, F32))
+        low_lane = lane_row < HD // 2
+        top = lax.fori_loop(0, n, lambda s, t: jnp.maximum(t, ml_in[s]), own_tile, unroll=n <= 8)
+        own_weight = jnp.where(low_lane, jnp.exp(own_tile - top), 0.0)
+
+        def merge(s, carry):
+            den, nums = carry
+            tile = ml_in[s]
+            factor = jnp.where(low_lane, jnp.exp(tile - top), 0.0)
+            part_rows = acc_in[s].astype(F32)
+            nums = [
+                num + part_rows[i * group : (i + 1) * group] * factor[:, i : i + 1]
+                for i, num in enumerate(nums)
+            ]
+            return den + pltpu.roll(tile, HD // 2, 1) * factor, nums
+
+        nums = [own_weight[:, i : i + 1] * own_values[i] for i in range(ipd)]
+        den, nums = lax.fori_loop(0, n, merge, (own_weight, nums), unroll=n <= 8)
         for i in range(ipd):
-            top = jnp.maximum(top_all[:, i : i + 1], own_scores[i])
-            own_weight = jnp.exp(own_scores[i] - top)
-            own_value = qg[me, i].astype(F32)[group + 1 : group + 2]
-
-            def merge(s, carry):
-                den, num = carry
-                tile = ml_in[s]
-                factor = jnp.exp(tile[:, i : i + 1] - top)
-                return den + tile[:, HD // 2 + i : HD // 2 + i + 1] * factor, num + acc_in[s, i] * factor
-
-            den, num = lax.fori_loop(
-                0, n, merge, (own_weight, own_weight * own_value), unroll=n <= 8
-            )
-            atf[i] = num / den
+            atf[i] = nums[i] / den[:, i : i + 1]
         for j in range(group):
             ats[:, j * HD : (j + 1) * HD] = atf[:, j, :].astype(BF16)
         atg[me] = ats[...]
@@ -356,7 +392,7 @@
 
         def reduce_and_send(d):
             dother_copy(d).wait_recv()
-            ssum[d] = dpart[hd, d] + dother[d]
+            ssum[d] = (dpart[hd, d] + dother[d]).astype(BF16)
             pool_copy(ssum.at[d], rsum.at[me], s8, r8, d).start()
 
         peers(reduce_and_send)
@@ -366,7 +402,7 @@
         def add_final(k, total):
             s = lax.rem(me + k, n)
             wait_from(ssum.at[s], rsum.at[s], s8, r8, s)
-            return total + rsum[s]
+            return total + rsum[s].astype(F32)
 
         final = lax.fori_loop(1, n, add_final, final)
         yb[hd] = (midf[hd] + final).astype(BF16)
@@ -418,22 +454,14 @@
     items = prompts * lh
     ipd = items // n
 
-    column = jnp.arange(HD) % (HD // 2)
-    inverse = jnp.exp(column.astype(F32) * (-2.0 * math.log(THETA) / HD))[None]
+    column = np.arange(HD) % (HD // 2)
+    exponent = column.astype(np.float32) * np.float32(-2.0 * math.log(THETA) / HD)
+    inverse = np.exp(exponent.astype(np.float64)).astype(np.float32)[None]
     first_end = HD // 8
     second_end = first_end + 3 * HD // 16
-    which = jnp.where(column < first_end, 0, jnp.where(column < second_end, 1, 2))
-    hit = (which[None] == jnp.arange(3)[:, None]).astype(F32)
-    pad = jnp.zeros((2, HD), F32)
-    sel = jnp.concatenate([64.0 * hit, hit, pad], 0).astype(BF16)
-    spread = jnp.transpose(positions, (1, 0, 2))
-    posx = jnp.concatenate(
-        [spread // 64, spread % 64, jnp.zeros((prompts, 2, seq), jnp.int32)], 1
-    ).astype(BF16)
-    qpos = query_pos.astype(F32)
-    qsel = jnp.where(
-        column < first_end, qpos[0][:, None], jnp.where(column < second_end, qpos[1][:, None], qpos[2][:, None])
-    )
+    which = np.where(column < first_end, 0, np.where(column < second_end, 1, 2))
+    hit = (which[None] == np.arange(3)[:, None]).astype(np.float32)
+    sel = jnp.asarray(np.concatenate([64.0 * hit, hit, np.zeros((2, HD), np.float32)], 0), BF16)
 
     kernel = make_kernel(n, prompts, lh, seq, d_model, ffl, group, wb, nslots, vslots, share)
     half = prompts // 2
@@ -441,7 +469,7 @@
     dma = pltpu.SemaphoreType.DMA
     scratch = [
         vm((prompts, lh, seq, HD), BF16),
-        vm((vslots, lh, seq, HD), BF16),
+        vm((vslots, ipd, seq, HD), BF16),
         vm((lh, cb, qw), BF16),
         vm(out_weight.shape, BF16),
         vm((ffl, d_model), BF16),
@@ -450,8 +478,8 @@
         vm((n, group + 2, ipd, HD), F32),
         vm((ipd, 16, HD), F32),
         vm((n, ipd, 16, HD), BF16),
-        vm((n, ipd, group, HD), F32),
-        vm((n, ipd, group, HD), F32),
+        vm((n, ipd * group, HD), BF16),
+        vm((n, ipd * group, HD), BF16),
         vm((n, group, HD), F32),
         vm((n, group, HD), F32),
         vm((ipd, group, HD), F32),
@@ -465,8 +493,8 @@
         vm((prompts, ffl), BF16),
         vm((2, n, half, cb), F32),
         vm((n, half, cb), F32),
-        vm((n, half, cb), F32),
-        vm((n, half, cb), F32),
+        vm((n, half, cb), BF16),
+        vm((n, half, cb), BF16),
         vm((2, half, cb), BF16),
         vm((2, prompts, HD), F32),
         dma((lh + 2,)),
@@ -489,7 +517,7 @@
             collective_id=0, has_side_effects=True, vmem_limit_bytes=67043328
         ),
     )(
-        hidden_in, posx, sel, qsel, inverse, lengths, key_cache, value_cache,
+        hidden_in, positions, query_pos, sel, jnp.asarray(inverse), lengths, key_cache, value_cache,
         query_weight, key_weight, value_weight, out_weight, gate_weight.T, up_weight.T, down_weight,
     )
 

time: 108 us -> 84.1 us (0.78)
  Pallas kernels: 102 us -> 82.5 us
  other arithmetic: 4.44 us -> 0 us
    pallas_call x1, Pallas kernels: 102 us -> 82.5 us  [per_device(): pl.pallas_call(kernel, out_shape=jax.ShapeDtypeStruct((prompts, cb), BF16...]
    concatenate x2 -> x0, other arithmetic: 1.37 us -> none  [the longest x1 0.73 us: per_device(): jnp.concatenate([spread // 64, spread % 64, jnp.zeros((prompts, 2, seq),...]
    another operation x3 -> x0, other arithmetic: 1.18 us -> none
where the time goes in v3:
time: 84.1 us; the launch traced here: 83.9 us
  Pallas kernels  82.5 us (98%)
  local copies, waits for them, and re-layouts  1.38 us (2%)
    pallas_call x1, Pallas kernels, per_device(): pl.pallas_call(kernel, out_shape=jax.ShapeDtypeStruct((prompts, cb), BF16...  82.5 us

profile of v3, /device:TPU:1, one launch (start us, length us, event | category | flops | bytes accessed | tf_op | source)
XLA Modules:
  0.0 83.9 jit_solution(12027706772440454996)
XLA Ops:
  0.0 82.5 %shard_map.145 = bf16[16,1024]{1,0:T(8,128)(2,1)} custom-call(bf16[16,8192]{1,0:T(8,128)(2,1)} %hidden.1, s32[3,16,512]{2,1,0:T(8,128)} %pos.1, s32[3,16]{1,0:T(4,128)} %qpos.1, bf16[8,128]{1,0:T(8,128)(2,1)} %constant.4.clone.sel, f32[1,128]{1,0:T(1,128)} %constant.5.clone.inv, s32[16]{0:T(128)} %lens.1, bf16[16,4,512,128]{3,2,1,0:T(8,128)(2,1)} %key_hbm.1, ...), custom_call_target="tpu_custom_call" | custom-call | tf_op jit(solution)/shard_map/pallas_call | solution.py:510
  82.5 1.4 %copy.17 = bf16[16,1024]{1,0:T(8,128)(2,1)} copy(bf16[16,1024]{1,0:T(8,128)(2,1)} %shard_map.145) | data formatting | bytes 65536
